TPU v7x, 32 devices: a whole 2x2x4 slice. The times are simulated.
32 devices in a mesh: dp: 8 (over z, x), mp: 4 (over y, core).
Axes of the slice: x: 2, y: 2, z: 4, core: 2. Of those that a mesh axis runs over, the one named last changes fastest.
Arguments:
- tokens: bfloat16 [8192, 2048], P('dp', 'mp'), may hold values from -6 to 6
- norm_gain: bfloat16 [2048], replicated, may hold values from 0.099609375 to 1.8984375
- wi_gate: bfloat16 [2048, 5120], P(None, 'mp'), may hold values from -0.125 to 0.125
- wi_linear: bfloat16 [2048, 5120], P(None, 'mp'), may hold values from -0.125 to 0.125
- wo_out: bfloat16 [5120, 2048], P('mp'), may hold values from -0.078125 to 0.078125
- task_table: float32 [8, 64], replicated, may hold values from -5 to 5
- layer_table: float32 [24, 64], replicated, may hold values from -5 to 5
- task_ids: int32 [64], P('dp'), may hold values from 0 to 7
- layer_index: int32 [1], replicated, may hold values from 0 to 23
- hyper_in: bfloat16 [128, 1024], P(None, 'mp'), may hold values from -0.5 to 0.5
- gen_down: bfloat16 [1024, 131072], P(None, ('mp', 'dp')), may hold values from -0.0078125 to 0.0078125
- gen_up: bfloat16 [1024, 131072], P(None, ('mp', 'dp')), may hold values from -0.046875 to 0.046875
Outputs:
- mixed: bfloat16 [8192, 2048], P('dp', 'mp')
All inputs are finite; a program needn't handle non-finite values.
Results may differ from a plain program's by a relative error of at most 0.019.
Values may be sent and summed in bfloat16 or wider, within the bound.
A program may use at most 128 MiB of HBM per device.

v0:
```python
import jax
import jax.numpy as jnp
from jax import lax
from jax.sharding import PartitionSpec as P

R = 64


def matmul(left, right):
    return jnp.dot(left, right, preferred_element_type=jnp.float32)


def per_device(
    tokens,
    norm_gain,
    wi_gate,
    wi_linear,
    wo_out,
    task_table,
    layer_table,
    task_ids,
    layer_index,
    hyper_in,
    gen_down,
    gen_up,
):
    task_count = task_table.shape[0]
    layer_row = jnp.take(layer_table, layer_index, axis=0)
    embed = jnp.concatenate(
        [task_table, jnp.broadcast_to(layer_row, (task_count, layer_row.shape[1]))], axis=1
    ).astype(jnp.bfloat16)
    hidden_part = jnp.maximum(matmul(embed, hyper_in), 0.0).astype(jnp.bfloat16)
    hidden = lax.all_gather(hidden_part, "mp", axis=1, tiled=True)
    every_id = lax.all_gather(task_ids, "dp", axis=0, tiled=True)
    wanted = jnp.take(hidden, every_id, axis=0)
    made = (
        matmul(wanted, gen_down).astype(jnp.bfloat16),
        matmul(wanted, gen_up).astype(jnp.bfloat16),
    )
    local_down, local_up = (
        lax.all_to_all(made[0], "dp", split_axis=0, concat_axis=1, tiled=True),
        lax.all_to_all(made[1], "dp", split_axis=0, concat_axis=1, tiled=True),
    )
    full_rows = lax.all_gather(tokens, "mp", axis=1, tiled=True)
    wide = full_rows.astype(jnp.float32)
    scale = lax.rsqrt(jnp.mean(wide * wide, axis=-1, keepdims=True) + 1e-06)
    normed = (wide * scale * norm_gain.astype(jnp.float32)).astype(jnp.bfloat16)
    gate = matmul(normed, wi_gate)
    linear = matmul(normed, wi_linear)
    act = (jax.nn.gelu(gate, approximate=True) * linear).astype(jnp.bfloat16)
    seqs_dev = task_ids.shape[0]
    tok_dev = tokens.shape[0]
    seq_len = tok_dev // seqs_dev
    partial_sums = matmul(act, wo_out)
    ffout = lax.psum_scatter(
        partial_sums.astype(jnp.bfloat16), "mp", scatter_dimension=1, tiled=True
    )
    down_block = local_down.reshape(seqs_dev, -1, R)
    up_block = local_up.reshape(seqs_dev, -1, R)
    blocks = ffout.reshape(seqs_dev, seq_len, -1)
    squeeze_part = jnp.einsum(
        "std,sdr->str", blocks, down_block, preferred_element_type=jnp.float32
    )
    squeeze_full = lax.psum(squeeze_part.astype(jnp.bfloat16), "mp").astype(jnp.float32)
    squeezed = jnp.maximum(squeeze_full, 0.0).astype(jnp.bfloat16)
    expand = jnp.einsum("str,sdr->std", squeezed, up_block, preferred_element_type=jnp.float32)
    total = tokens.astype(jnp.float32) + ffout.astype(jnp.float32) + expand.reshape(tok_dev, -1)
    return total.astype(jnp.bfloat16)


def solution(mesh):
    return jax.shard_map(
        per_device,
        mesh=mesh,
        in_specs=(
            P("dp", "mp"),
            P(),
            P(None, "mp"),
            P(None, "mp"),
            P("mp", None),
            P(),
            P(),
            P("dp"),
            P(),
            P(None, "mp"),
            P(None, ("mp", "dp")),
            P(None, ("mp", "dp")),
        ),
        out_specs=P("dp", "mp"),
        check_vma=False,
    )
```

profile of v0, /device:TPU:0, one launch (start us, length us, event | category | flops | bytes accessed | tf_op | source)
XLA Modules:
  0.0 174.6 jit_solution(7065484068272233757)
XLA Ops:
  6.5 0.7 all-gather.2.cloned.1.call-update
  7.3 0.0 reduce-scatter.2.cloned.1.call-start
  7.3 0.7 convert_element_type.45
  8.0 38.1 %all-gather.2.cloned.1.call-done = bf16[1024,2048]{1,0:T(8,128)(2,1)} async-done(((bf16[1024,512]{1,0:T(8,128)(2,1)}), bf16[1024,2048]{1,0:T(8,128)(2,1)}) %all-gather.2.cloned.1.call-update) | async-done | bytes 4194320 | tf_op jit(solution)/shard_map/all_gather | solution.py:44
  46.1 3.1 %fusion = f32[1024]{0:T(1024)S(1)} fusion(bf16[1024,2048]{1,0:T(8,128)(2,1)} %all-gather.2.cloned.1.call-done), kind=kLoop, calls=%fused_computation.3 | loop fusion | flops 6290432 | bytes 4198400 | tf_op jit(solution)/shard_map/reduce_sum | solution.py:46
  49.2 10.7 %fusion.16 = f32[1024,1280]{1,0:T(8,128)} fusion(bf16[2048,1280]{1,0:T(8,128)(2,1)} %param.14, bf16[1024,2048]{1,0:T(8,128)(2,1)} %all-gather.2.cloned.1.call-done, f32[2048]{0:T(1024)S(1)} %convert_element_type.45, f32[1024]{0:T(1024)S(1)} %add_rsqrt_fusion), kind=kOutput, calls=%fused_computation.23 | convolution fusion | flops 5377097728 | bytes 14692352 | tf_op jit(solution)/shard_map/dot_general | solution.py:10
  59.9 19.9 %convolution_convert_fusion.2 = bf16[1024,2048]{1,0:T(8,128)(2,1)} fusion(bf16[1280,2048]{1,0:T(8,128)(2,1)} %param.16, f32[1024,1280]{1,0:T(8,128)} %fusion.16, bf16[2048,1280]{1,0:T(8,128)(2,1)} %param.15, bf16[1024,2048]{1,0:T(8,128)(2,1)} %all-gather.2.cloned.1.call-done, f32[2048]{0:T(1024)S(1)} %convert_element_type.45, f32[1024]{0:T(1024)S(1)} %add_rsqrt_fusion), kind=kOutput, calls=%fused_computation.20 | convolution fusion | flops 10761011200 | bytes 24129536 | tf_op jit(solution)/shard_map/dot_general | solution.py:10
  79.8 0.0 reduce-scatter.2.cloned.1.call-update
  80.5 0.7 fusion.27
  81.2 0.1 pad.3.clone
  81.3 0.6 dynamic-slice.4
  82.6 0.2 dynamic-update-slice.1
  82.8 11.4 %all-reduce = s32[64]{0:T(128)S(1)} all-reduce(s32[64]{0:T(128)S(1)} %dynamic-update-slice.1), channel_id=1, replica_groups=mesh['dp'=8,'mp'=4] {'dp'}, use_global_device_ids=true, to_apply=%add | all-reduce | flops 64 | bytes 512
  94.2 0.1 fusion.18
  94.3 5.2 %all_gather.11 = bf16[8,1024]{1,0:T(8,128)(2,1)S(1)} all-gather(bf16[8,256]{1,0:T(8,128)(2,1)S(1)} %fusion.18), channel_id=1, replica_groups=mesh['dp'=8,'mp'=4] {'mp'}, dimensions={1}, use_global_device_ids=true | all-gather | bytes 20480 | tf_op jit(solution)/shard_map/all_gather | solution.py:33
  99.5 0.7 gather_fusion
  100.2 5.8 %fusion.12 = bf16[8,8,4096]{2,1,0:T(8,128)(2,1)} fusion(bf16[1024,4096]{1,0:T(8,128)(2,1)} %param.22, bf16[64,1024]{1,0:T(8,128)(2,1)S(1)} %gather_fusion, pred[64]{0:T(512)(128)(4,1)S(1)} %compare_and_fusion), kind=kOutput, calls=%fused_computation.18 | convolution fusion | flops 537198592 | bytes 9044032 | tf_op jit(solution)/shard_map/dot_general | solution.py:10
  106.1 3.5 %all-to-all-start = ((bf16[8,8,4096]{2,1,0:T(8,128)(2,1)}), bf16[8,8,4096]{2,1,0:T(8,128)(2,1)S(1)}, u32[]{:S(2)}, u32[]{:S(2)}) async-start(bf16[8,8,4096]{2,1,0:T(8,128)(2,1)} %fusion.12), calls=%async_computation.1 | async-start | bytes 1048576 | tf_op jit(solution)/shard_map/all_to_all | solution.py:41
  109.6 5.8 %fusion.13 = bf16[8,8,4096]{2,1,0:T(8,128)(2,1)} fusion(bf16[1024,4096]{1,0:T(8,128)(2,1)} %param.23, bf16[64,1024]{1,0:T(8,128)(2,1)S(1)} %gather_fusion, pred[64]{0:T(512)(128)(4,1)S(1)} %compare_and_fusion), kind=kOutput, calls=%fused_computation.19 | convolution fusion | flops 537198592 | bytes 9044032 | tf_op jit(solution)/shard_map/dot_general | solution.py:10
  115.4 9.4 %all-to-all-done = bf16[8,8,4096]{2,1,0:T(8,128)(2,1)S(1)} async-done(((bf16[8,8,4096]{2,1,0:T(8,128)(2,1)}), bf16[8,8,4096]{2,1,0:T(8,128)(2,1)S(1)}, u32[]{:S(2)}, u32[]{:S(2)}) %all-to-all-start) | async-done | bytes 524320 | tf_op jit(solution)/shard_map/all_to_all | solution.py:41
  124.8 4.3 %all-to-all-start.1 = ((bf16[8,8,4096]{2,1,0:T(8,128)(2,1)}), bf16[8,8,4096]{2,1,0:T(8,128)(2,1)}, u32[]{:S(2)}, u32[]{:S(2)}) async-start(bf16[8,8,4096]{2,1,0:T(8,128)(2,1)} %fusion.13), calls=%async_computation.2 | async-start | bytes 1048576 | tf_op jit(solution)/shard_map/all_to_all | solution.py:42
  129.1 0.0 all-reduce.3.cloned.1.call-start
  129.1 0.3 copy.16
  129.4 1.1 reshape.46
  130.6 0.0 reduce-scatter.2.cloned.1.call-done
  130.6 2.5 %convolution_convert_fusion.3 = bf16[8,128,64]{1,2,0:T(8,128)(2,1)} fusion(bf16[8,128,512]{2,1,0:T(8,128)(2,1)} %bitcast.25, bf16[8,512,64]{2,1,0:T(8,128)(2,1)S(1)} %reshape.46), kind=kOutput, calls=%fused_computation.24 | convolution fusion | flops 67174400 | bytes 1703936 | tf_op jit(solution)/shard_map/std,sdr->str/dot_general | solution.py:61
  133.1 10.2 %all-to-all-done.1 = bf16[8,8,4096]{2,1,0:T(8,128)(2,1)} async-done(((bf16[8,8,4096]{2,1,0:T(8,128)(2,1)}), bf16[8,8,4096]{2,1,0:T(8,128)(2,1)}, u32[]{:S(2)}, u32[]{:S(2)}) %all-to-all-start.1) | async-done | bytes 524320 | tf_op jit(solution)/shard_map/all_to_all | solution.py:42
  143.3 2.1 %copy.18 = bf16[8,8,4096]{2,1,0:T(8,128)(2,1)} copy(bf16[8,8,4096]{2,0,1:T(8,128)(2,1)} %bitcast.8) | data formatting | bytes 1048576 | tf_op jit(solution)/shard_map/all_to_all | solution.py:42
  145.4 2.1 %reshape.47 = bf16[8,512,64]{2,1,0:T(8,128)(2,1)S(1)} reshape(bf16[8,8,4096]{2,1,0:T(8,128)(2,1)} %copy.18) | data formatting | bytes 1048576 | tf_op jit(solution)/shard_map/reshape | solution.py:59
  147.5 17.7 %all-reduce.3.cloned.1.call-done = bf16[8,128,64]{1,2,0:T(8,128)(2,1)} async-done(((bf16[8,128,64]{1,2,0:T(8,128)(2,1)}), bf16[8,128,64]{1,2,0:T(8,128)(2,1)}) %all-reduce.3.cloned.1.call-update) | async-done | bytes 131088 | tf_op jit(solution)/shard_map/psum | solution.py:64
  165.2 1.4 fusion.21
  166.6 1.4 fusion.14
  (20 shorter events, 0.1 us)
Async XLA Ops:
  6.5 87.6 %copy-start = (bf16[128,256]{1,0:T(8,128)(2,1)S(1)}, bf16[128,256]{1,0:T(8,128)(2,1)}, u32[]{:S(2)}) copy-start(bf16[128,256]{1,0:T(8,128)(2,1)} %param.21) | copy-start | bytes 196612
  6.5 39.6 %all-gather.2.cloned.1.call-start = ((), (), s32[]{:S(2)}) async-start(), calls=%async_computation.3 | async-start | bytes 5242880 | tf_op jit(solution)/shard_map/all_gather | solution.py:44
  7.3 123.3 %reduce-scatter.2.cloned.1.call-start = ((), (), s32[]{:S(2)}) async-start(), calls=%async_computation.4 | async-start | bytes 5242880 | tf_op jit(solution)/shard_map/reduce_scatter | solution.py:55
  59.9 20.6 %copy-start.3 = (f32[8,64]{1,0:T(8,128)S(1)}, f32[8,64]{1,0:T(8,128)}, u32[]{:S(2)}) copy-start(f32[8,64]{1,0:T(8,128)} %param.17) | copy-start | bytes 6148
  59.9 21.4 %copy-start.5 = (u32[32]{0:T(128)S(1)}, u32[32]{0:T(128)}, u32[]{:S(2)}) copy-start(u32[32]{0:T(128)} %constant.73) | copy-start | bytes 388
  59.9 22.7 %copy-start.4 = (s32[8]{0:T(128)S(1)}, s32[8]{0:T(128)}, u32[]{:S(2)}) copy-start(s32[8]{0:T(128)} %param.19) | copy-start | bytes 100
  106.1 18.7 %all-to-all-start = ((bf16[8,8,4096]{2,1,0:T(8,128)(2,1)}), bf16[8,8,4096]{2,1,0:T(8,128)(2,1)S(1)}, u32[]{:S(2)}, u32[]{:S(2)}) async-start(bf16[8,8,4096]{2,1,0:T(8,128)(2,1)} %fusion.12), calls=%async_computation.1 | async-start | bytes 1048576 | tf_op jit(solution)/shard_map/all_to_all | solution.py:41
  124.8 18.6 %all-to-all-start.1 = ((bf16[8,8,4096]{2,1,0:T(8,128)(2,1)}), bf16[8,8,4096]{2,1,0:T(8,128)(2,1)}, u32[]{:S(2)}, u32[]{:S(2)}) async-start(bf16[8,8,4096]{2,1,0:T(8,128)(2,1)} %fusion.13), calls=%async_computation.2 | async-start | bytes 1048576 | tf_op jit(solution)/shard_map/all_to_all | solution.py:42
  129.1 36.1 %all-reduce.3.cloned.1.call-start = ((), (), s32[]{:S(2)}) async-start(), calls=%async_computation.5 | async-start | bytes 262144 | tf_op jit(solution)/shard_map/psum | solution.py:64
  129.1 37.5 %copy-start.1 = (bf16[1024,512]{1,0:T(8,128)(2,1)S(1)}, bf16[1024,512]{1,0:T(8,128)(2,1)}, u32[]{:S(2)}) copy-start(bf16[1024,512]{1,0:T(8,128)(2,1)} %param.12) | copy-start | bytes 3145732
  130.6 36.0 %copy-start.2 = (bf16[1024,512]{1,0:T(8,128)(2,1)S(1)}, bf16[1024,512]{1,0:T(8,128)(2,1)}, u32[]{:S(2)}) copy-start(bf16[1024,512]{1,0:T(8,128)(2,1)} %reduce-scatter.2.cloned.1.call-done) | copy-start | bytes 3145732
Sparse Core Ops, SparseCore 0:
  8.9 37.1 all-gather.1
  80.0 44.3 reduce-scatter.1
  133.2 31.9 all-reduce.2
where the time goes:
time: 175 us
  waiting for transfers between devices  76.2 us (44%)
  matrix products  46.2 us (26%)
  blocking collectives  16.6 us (9%)
  between operations  14.6 us (8%)
  starting transfers between devices  7.9 us (5%)
  local copies, waits for them, and re-layouts  7.23 us (4%)
  other arithmetic  5.92 us (3%)
    dot_general x5, matrix products, matmul(): return jnp.dot(left, right, preferred_element_type=jnp.float32)  42.4 us
    all_gather x1, waiting for transfers between devices, per_device(): full_rows = lax.all_gather(tokens, 'mp', axis=1, tiled=True)  38.1 us
    psum x1, waiting for transfers between devices, per_device(): lax.psum(squeeze_part.astype(jnp.bfloat16), 'mp').astype(jnp.float32)  17.7 us
    unnamed x1, blocking collectives  11.4 us
    all_to_all x1, waiting for transfers between devices, per_device(): lax.all_to_all(made[1], 'dp', split_axis=0, concat_axis=1, tiled=True)  10.2 us
    all_to_all x1, waiting for transfers between devices, per_device(): lax.all_to_all(made[0], 'dp', split_axis=0, concat_axis=1, tiled=True)  9.39 us
    all_gather x1, blocking collectives, per_device(): hidden = lax.all_gather(hidden_part, 'mp', axis=1, tiled=True)  5.2 us
    all_to_all x1, starting transfers between devices, per_device(): lax.all_to_all(made[1], 'dp', split_axis=0, concat_axis=1, tiled=True)  4.33 us
  transfers between devices with their start and end apart: 5, of which 4 were waited for; matrix products, arithmetic and copies ran while one was open for 13% of the time, Pallas kernels for 0%

commit v1 on v0

--- a/solution.py
+++ b/solution.py
@@ -4,6 +4,13 @@
 from jax.sharding import PartitionSpec as P
 
 R = 64
+
+
+def trade_parts(x, axis, split, join):
+    size = lax.axis_size(axis)
+    blocks = jnp.stack(jnp.split(x, size, axis=split), axis=0)
+    blocks = lax.all_to_all(blocks, axis, split_axis=0, concat_axis=0)
+    return jnp.concatenate(blocks, axis=join)
 
 
 def matmul(left, right):
@@ -38,7 +45,7 @@
         matmul(wanted, gen_up).astype(jnp.bfloat16),
     )
     local_down, local_up = (
-        lax.all_to_all(made[0], "dp", split_axis=0, concat_axis=1, tiled=True),
+        trade_parts(made[0], "dp", 0, 1),
         lax.all_to_all(made[1], "dp", split_axis=0, concat_axis=1, tiled=True),
     )
     full_rows = lax.all_gather(tokens, "mp", axis=1, tiled=True)

time: 175 us -> 169 us (0.966)
  waiting for transfers between devices: 76.2 us -> 59.7 us
  local copies, waits for them, and re-layouts: 7.23 us -> 13.5 us
  starting transfers between devices: 7.9 us -> 9.93 us
  blocking collectives: 16.6 us -> 18.5 us
    all_gather x1, waiting for transfers between devices: 38.1 us -> 8.93 us  [per_device(): full_rows = lax.all_gather(tokens, 'mp', axis=1, tiled=True)]
    reduce_scatter x1, waiting for transfers between devices: 0.02 us -> 13.3 us  [per_device(): lax.psum_scatter(partial_sums.astype(jnp.bfloat16), 'mp', scatter_dimensi...]
    all_to_all x1, waiting for transfers between devices: 10.2 us -> 0.01 us  [per_device(): lax.all_to_all(made[1], 'dp', split_axis=0, concat_axis=1, tiled=True)]
    psum x1, waiting for transfers between devices: 17.7 us -> 27.7 us  [per_device(): lax.psum(squeeze_part.astype(jnp.bfloat16), 'mp').astype(jnp.float32)]
    unnamed x15 -> x16, local copies, waits for them, and re-layouts: 0.85 us -> 6.51 us
    all_to_all x1, starting transfers between devices: 3.49 us -> 5.51 us  [trade_parts(): blocks = lax.all_to_all(blocks, axis, split_axis=0, concat_axis=0)]
    another operation x0 -> x2, local copies, waits for them, and re-layouts: none -> 1.75 us  [the longest x1 1.12 us: per_device(): down_block = local_down.reshape(seqs_dev, -1, R)]
  transfers between devices with their start and end apart: 5 -> 5, of which waited for: 4 -> 4; matrix products, arithmetic and copies ran while one was open for 13% -> 17% of each run, Pallas kernels for 0% -> 0%
where the time goes in v1:
time: 169 us; the launch traced here: 168 us
  waiting for transfers between devices  59.7 us (35%)
  matrix products  45.6 us (27%)
  blocking collectives  18.5 us (11%)
  between operations  14.5 us (9%)
  local copies, waits for them, and re-layouts  13.5 us (8%)
  starting transfers between devices  9.93 us (6%)
  other arithmetic  6.59 us (4%)
    dot_general x5, matrix products, matmul(): return jnp.dot(left, right, preferred_element_type=jnp.float32)  41.7 us
    psum x1, waiting for transfers between devices, per_device(): lax.psum(squeeze_part.astype(jnp.bfloat16), 'mp').astype(jnp.float32)  27.7 us
    reduce_scatter x1, waiting for transfers between devices, per_device(): lax.psum_scatter(partial_sums.astype(jnp.bfloat16), 'mp', scatter_dimensi...  13.3 us
    unnamed x1, blocking collectives  13.1 us
    all_to_all x1, waiting for transfers between devices, trade_parts(): blocks = lax.all_to_all(blocks, axis, split_axis=0, concat_axis=0)  8.98 us
    all_gather x1, waiting for transfers between devices, per_device(): full_rows = lax.all_gather(tokens, 'mp', axis=1, tiled=True)  8.93 us
    unnamed x16, local copies, waits for them, and re-layouts  6.51 us
    all_to_all x1, starting transfers between devices, trade_parts(): blocks = lax.all_to_all(blocks, axis, split_axis=0, concat_axis=0)  5.51 us
  transfers between devices with their start and end apart: 5, of which 4 were waited for; matrix products, arithmetic and copies ran while one was open for 17% of the time, Pallas kernels for 0%

profile of v1, /device:TPU:0, one launch (start us, length us, event | category | flops | bytes accessed | tf_op | source)
XLA Modules:
  0.0 168.3 jit_solution(17253520479198952439)
XLA Ops:
  6.5 0.7 all-gather.2.cloned.1.call-update
  8.0 0.7 convert.7
  8.7 0.7 convert_element_type.45
  9.3 0.7 fusion.34
  10.1 1.2 dynamic-slice.4
  12.0 0.9 dynamic-update-slice.1
  12.9 13.1 %all-reduce = s32[64]{0:T(128)S(1)} all-reduce(s32[64]{0:T(128)S(1)} %dynamic-update-slice.1), channel_id=1, replica_groups=mesh['dp'=8,'mp'=4] {'dp'}, use_global_device_ids=true, to_apply=%add | all-reduce | flops 64 | bytes 512
  26.1 5.4 %all_gather.11 = bf16[8,1024]{1,0:T(8,128)(2,1)S(1)} all-gather(bf16[8,256]{1,0:T(8,128)(2,1)S(1)} %fusion.17), channel_id=1, replica_groups=mesh['dp'=8,'mp'=4] {'mp'}, dimensions={1}, use_global_device_ids=true | all-gather | bytes 20480 | tf_op jit(solution)/shard_map/all_gather | solution.py:40
  31.5 0.7 gather_fusion
  32.2 5.1 %convolution_convert_fusion.1 = bf16[64,4096]{1,0:T(8,128)(2,1)S(1)} fusion(bf16[1024,4096]{1,0:T(8,128)(2,1)} %param.22, bf16[64,1024]{1,0:T(8,128)(2,1)S(1)} %gather_fusion, pred[64]{0:T(512)(128)(4,1)S(1)} %compare_and_fusion), kind=kOutput, calls=%fused_computation.17 | convolution fusion | flops 537198592 | bytes 9044032 | tf_op jit(solution)/shard_map/dot_general | solution.py:17
  37.3 8.9 %all-gather.2.cloned.1.call-done = bf16[1024,2048]{1,0:T(8,128)(2,1)} async-done(((bf16[1024,512]{1,0:T(8,128)(2,1)}), bf16[1024,2048]{1,0:T(8,128)(2,1)}) %all-gather.2.cloned.1.call-update) | async-done | bytes 4194320 | tf_op jit(solution)/shard_map/all_gather | solution.py:51
  46.2 3.1 %fusion = f32[1024]{0:T(1024)S(1)} fusion(bf16[1024,2048]{1,0:T(8,128)(2,1)} %all-gather.2.cloned.1.call-done), kind=kLoop, calls=%fused_computation.3 | loop fusion | flops 6290432 | bytes 4198400 | tf_op jit(solution)/shard_map/reduce_sum | solution.py:53
  49.3 10.7 %fusion.15 = f32[1024,1280]{1,0:T(8,128)} fusion(bf16[2048,1280]{1,0:T(8,128)(2,1)} %param.14, bf16[1024,2048]{1,0:T(8,128)(2,1)} %all-gather.2.cloned.1.call-done, f32[2048]{0:T(1024)S(1)} %convert_element_type.45, f32[1024]{0:T(1024)S(1)} %add_rsqrt_fusion), kind=kOutput, calls=%fused_computation.22 | convolution fusion | flops 5377097728 | bytes 14692352 | tf_op jit(solution)/shard_map/dot_general | solution.py:17
  60.0 19.9 %convolution_convert_fusion.2 = bf16[1024,2048]{1,0:T(8,128)(2,1)} fusion(bf16[1280,2048]{1,0:T(8,128)(2,1)} %param.16, f32[1024,1280]{1,0:T(8,128)} %fusion.15, bf16[2048,1280]{1,0:T(8,128)(2,1)} %param.15, bf16[1024,2048]{1,0:T(8,128)(2,1)} %all-gather.2.cloned.1.call-done, f32[2048]{0:T(1024)S(1)} %convert_element_type.45, f32[1024]{0:T(1024)S(1)} %add_rsqrt_fusion), kind=kOutput, calls=%fused_computation.19 | convolution fusion | flops 10761011200 | bytes 24129536 | tf_op jit(solution)/shard_map/dot_general | solution.py:17
  79.9 0.6 fusion.29
  80.5 0.6 fusion.28
  81.2 0.6 fusion.27
  83.1 0.6 fusion.24
  83.7 0.6 fusion.23
  84.3 0.6 fusion.22
  85.0 5.5 %all-to-all-start = ((bf16[8,8,4096]{2,1,0:T(8,128)(2,1)}), bf16[8,8,4096]{2,1,0:T(8,128)(2,1)S(1)}, u32[]{:S(2)}, u32[]{:S(2)}) async-start(bf16[8,8,4096]{2,1,0:T(8,128)(2,1)} %fusion.22), calls=%async_computation.1 | async-start | bytes 1048576 | tf_op jit(solution)/shard_map/all_to_all | solution.py:12
  90.5 5.9 %fusion.12 = bf16[8,8,4096]{2,1,0:T(8,128)(2,1)} fusion(bf16[1024,4096]{1,0:T(8,128)(2,1)} %param.23, bf16[64,1024]{1,0:T(8,128)(2,1)S(1)} %gather_fusion, pred[64]{0:T(512)(128)(4,1)S(1)} %compare_and_fusion), kind=kOutput, calls=%fused_computation.18 | convolution fusion | flops 537198592 | bytes 9044032 | tf_op jit(solution)/shard_map/dot_general | solution.py:17
  96.4 9.0 %all-to-all-done = bf16[8,8,4096]{2,1,0:T(8,128)(2,1)S(1)} async-done(((bf16[8,8,4096]{2,1,0:T(8,128)(2,1)}), bf16[8,8,4096]{2,1,0:T(8,128)(2,1)S(1)}, u32[]{:S(2)}, u32[]{:S(2)}) %all-to-all-start) | async-done | bytes 524320 | tf_op jit(solution)/shard_map/all_to_all | solution.py:12
  105.3 4.3 %all-to-all-start.1 = ((bf16[8,8,4096]{2,1,0:T(8,128)(2,1)}), bf16[8,8,4096]{2,1,0:T(8,128)(2,1)}, u32[]{:S(2)}, u32[]{:S(2)}) async-start(bf16[8,8,4096]{2,1,0:T(8,128)(2,1)} %fusion.12), calls=%async_computation.2 | async-start | bytes 1048576 | tf_op jit(solution)/shard_map/all_to_all | solution.py:49
  110.0 1.1 reshape_reshape.3
  111.2 13.3 %reduce-scatter.2.cloned.1.call-done = bf16[1024,512]{1,0:T(8,128)(2,1)} async-done(((bf16[1024,2048]{1,0:T(8,128)(2,1)}), bf16[1024,512]{1,0:T(8,128)(2,1)}) %reduce-scatter.2.cloned.1.call-update) | async-done | bytes 1048592 | tf_op jit(solution)/shard_map/reduce_scatter | solution.py:62
  124.5 2.5 %convolution_convert_fusion.3 = bf16[8,128,64]{1,2,0:T(8,128)(2,1)} fusion(bf16[8,128,512]{2,1,0:T(8,128)(2,1)} %bitcast.55, bf16[8,512,64]{2,1,0:T(8,128)(2,1)S(1)} %reshape_reshape.3), kind=kOutput, calls=%fused_computation.23 | convolution fusion | flops 67174400 | bytes 1703936 | tf_op jit(solution)/shard_map/std,sdr->str/dot_general | solution.py:68
  127.0 2.1 %copy.18 = bf16[8,8,4096]{2,1,0:T(8,128)(2,1)} copy(bf16[8,8,4096]{2,0,1:T(8,128)(2,1)} %bitcast.15) | data formatting | bytes 1048576 | tf_op jit(solution)/shard_map/all_to_all | solution.py:49
  129.1 2.1 %reshape.43 = bf16[8,512,64]{2,1,0:T(8,128)(2,1)S(1)} reshape(bf16[8,8,4096]{2,1,0:T(8,128)(2,1)} %copy.18) | data formatting | bytes 1048576 | tf_op jit(solution)/shard_map/reshape | solution.py:66
  131.2 27.7 %all-reduce.3.cloned.1.call-done = bf16[8,128,64]{1,2,0:T(8,128)(2,1)} async-done(((bf16[8,128,64]{1,2,0:T(8,128)(2,1)}), bf16[8,128,64]{1,2,0:T(8,128)(2,1)}) %all-reduce.3.cloned.1.call-update) | async-done | bytes 131088 | tf_op jit(solution)/shard_map/psum | solution.py:71
  158.9 1.4 fusion.20
  160.3 1.4 fusion.13
  (22 shorter events, 1.9 us)
Async XLA Ops:
  6.5 19.4 %copy-start = (bf16[128,256]{1,0:T(8,128)(2,1)S(1)}, bf16[128,256]{1,0:T(8,128)(2,1)}, u32[]{:S(2)}) copy-start(bf16[128,256]{1,0:T(8,128)(2,1)} %param.21) | copy-start | bytes 196612
  6.5 39.7 %all-gather.2.cloned.1.call-start = ((), (), s32[]{:S(2)}) async-start(), calls=%async_computation.3 | async-start | bytes 5242880 | tf_op jit(solution)/shard_map/all_gather | solution.py:51
  7.3 117.2 %reduce-scatter.2.cloned.1.call-start = ((), (), s32[]{:S(2)}) async-start(), calls=%async_computation.4 | async-start | bytes 5242880 | tf_op jit(solution)/shard_map/reduce_scatter | solution.py:62
  85.0 20.4 %all-to-all-start = ((bf16[8,8,4096]{2,1,0:T(8,128)(2,1)}), bf16[8,8,4096]{2,1,0:T(8,128)(2,1)S(1)}, u32[]{:S(2)}, u32[]{:S(2)}) async-start(bf16[8,8,4096]{2,1,0:T(8,128)(2,1)} %fusion.22), calls=%async_computation.1 | async-start | bytes 1048576 | tf_op jit(solution)/shard_map/all_to_all | solution.py:12
  105.3 21.6 %all-to-all-start.1 = ((bf16[8,8,4096]{2,1,0:T(8,128)(2,1)}), bf16[8,8,4096]{2,1,0:T(8,128)(2,1)}, u32[]{:S(2)}, u32[]{:S(2)}) async-start(bf16[8,8,4096]{2,1,0:T(8,128)(2,1)} %fusion.12), calls=%async_computation.2 | async-start | bytes 1048576 | tf_op jit(solution)/shard_map/all_to_all | solution.py:49
  109.7 49.2 %all-reduce.3.cloned.1.call-start = ((), (), s32[]{:S(2)}) async-start(), calls=%async_computation.5 | async-start | bytes 262144 | tf_op jit(solution)/shard_map/psum | solution.py:71
  109.7 50.5 %copy-start.1 = (bf16[1024,512]{1,0:T(8,128)(2,1)S(1)}, bf16[1024,512]{1,0:T(8,128)(2,1)}, u32[]{:S(2)}) copy-start(bf16[1024,512]{1,0:T(8,128)(2,1)} %param.12) | copy-start | bytes 3145732
  124.5 35.8 %copy-start.2 = (bf16[1024,512]{1,0:T(8,128)(2,1)S(1)}, bf16[1024,512]{1,0:T(8,128)(2,1)}, u32[]{:S(2)}) copy-start(bf16[1024,512]{1,0:T(8,128)(2,1)} %reduce-scatter.2.cloned.1.call-done) | copy-start | bytes 3145732
Sparse Core Ops, SparseCore 0:
  8.9 37.2 all-gather.1
  80.0 44.3 reduce-scatter.1
  127.1 31.7 all-reduce.2
